TPU v7x, 512 devices: a 4x2x32 block of a 4x8x32 slice. The times are simulated.
512 devices in a mesh: groups: 2 (over y), rows: 32 (over z), keys: 4 (over x), heads: 2 (over core).
Axes of the slice: x: 4, y: 2, z: 32, core: 2. Of those that a mesh axis runs over, the one named last changes fastest.
The devices are a block of a 4x8x32 slice.
Arguments:
- pair: bfloat16 [2048, 1024, 128], P(('groups', 'rows'), 'keys'), parts along dimension 0, may hold values from -6 to 6
- seq_length: int32 [2], P('groups'), parts along dimension 0, may hold values from 513 to 1024
- tile_counts: int32 [2048, 8], P(('groups', 'rows')), parts along dimension 0, may hold values from 0 to 128, as said below
- ln_gain: float32 [128], replicated, may hold values from 0.5 to 1.5
- w_query: bfloat16 [128, 128], P(None, 'heads'), may hold values from -8 to 8
- w_key: bfloat16 [128, 128], P(None, 'heads'), may hold values from -0.5 to 0.5
- w_value: bfloat16 [128, 128], P(None, 'heads'), may hold values from -0.5 to 0.5
- w_gate: bfloat16 [128, 128], P(None, 'heads'), may hold values from -0.5 to 0.5
- w_bias: bfloat16 [128, 4], P(None, 'heads'), may hold values from -1.5 to 1.5
- w_out: bfloat16 [128, 128], replicated, may hold values from -2 to 2
Outputs:
- update: bfloat16 [2048, 1024, 128], P(('groups', 'rows'), ('keys', 'heads')), parts along dimension 0
There are 2 independent parts, one for each index of `groups`. A program takes and returns all parts, laid end to end along the dimension named above; an argument that names none is the same for every part. Nothing has to cross between parts.
Inputs may be any that keep to these rules, and one draw needn't show every extreme that they name: `tile_counts`: for each row and each tile of 128 keys, how many of the tile's leading keys are valid; some rows have no valid key at all.
All inputs are finite; a program needn't handle non-finite values.
Results may differ from a plain program's by a relative error of at most 0.03.
The roundings to bfloat16 on the way count: a program that leaves them out, or rounds other values in their place, can miss the bound.
Values may be sent and summed in bfloat16 or wider, within the bound.
No kernel may reach another device: no remote copies, remote signals or barrier semaphores. Data moves between devices by JAX's collectives and lax.ppermute only.
A program may use at most 128 MiB of HBM per device.

v0:
```python
import functools

import jax
import jax.numpy as jnp
from jax import lax
from jax.experimental import pallas as pl
from jax.experimental.pallas import tpu as pltpu
from jax.sharding import PartitionSpec as P


HEAD_DIM = 32
TILE = 128
NORM_EPSILON = 1e-05
MASKED = -1e30
FLOOR = -1e29
SEGMENT = 8
STEP = 8
LOG2E = 1.4426950408889634
NORM_VMEM = 20
PROJECT_VMEM = 20
ATTEND_VMEM = 32


def shift(size, by):
    return [(i, (i + by) % size) for i in range(size)]


def contract_lanes(a, b):
    return lax.dot_general(a, b, (((1,), (1,)), ((), ())), preferred_element_type=jnp.float32)


def norm_kernel(scalars, pair_ref, gain_ref, wb_ref, half_ref, bias_ref, bias_scr):
    gain = gain_ref[...]
    ones = jnp.full((128, 128), 1.0 / 128, jnp.bfloat16)
    wb = wb_ref[...]
    rows, cols, channels = pair_ref.shape
    group = 4
    for at in range(0, rows, group):
        raw = pair_ref[at : at + group].reshape(group * cols, channels)
        mean = jnp.dot(raw, ones, preferred_element_type=jnp.float32)
        center = raw.astype(jnp.float32) - mean
        spread = jnp.mean(center * center, axis=-1, keepdims=True)
        normed = (center * lax.rsqrt(spread + NORM_EPSILON) * gain).astype(jnp.bfloat16)

        @pl.when(pl.program_id(0) == 0)
        def _():
            half_ref[at : at + group] = normed.reshape(group, cols, channels)

        b = contract_lanes(wb, normed)
        for r in range(group):
            for h in range(2):
                bias_scr[h, at + r : at + r + 1, :] = b[h : h + 1, r * cols : (r + 1) * cols]
    bias_ref[...] = bias_scr[...].astype(jnp.bfloat16)


def project_queries(own_ref, pack, q_ref, g_ref):
    rows, cols, channels = own_ref.shape
    own = own_ref[...].reshape(rows * cols, channels)
    qg = jnp.dot(own, pack[:, :256], preferred_element_type=jnp.float32)
    q = (qg[:, :128] * HEAD_DIM**-0.5).astype(jnp.bfloat16).astype(jnp.float32) * LOG2E
    high = q.astype(jnp.bfloat16)
    low = (q - high.astype(jnp.float32)).astype(jnp.bfloat16)
    lane = lax.broadcasted_iota(jnp.int32, (1, 128), 1)
    q_ref[...] = jnp.where(lane < 64, high, low).reshape(own_ref.shape)
    g_ref[...] = jax.nn.sigmoid(qg[:, 128:]).reshape(own_ref.shape)


def project_keys(sources, pack, k_ref, v_ref):
    for at, ref in enumerate(sources):
        rows, cols, channels = ref.shape
        span = slice(at * cols, (at + 1) * cols)
        block = ref[...].reshape(rows * cols, channels)
        v = jnp.dot(block, pack[:, 256:384], preferred_element_type=jnp.float32)
        v_ref[:, span, :] = v.astype(jnp.bfloat16).reshape(ref.shape)
        k = contract_lanes(pack[:64, 384:], block).astype(jnp.bfloat16)
        for r in range(rows):
            k_ref[r, :, span] = k[:, r * cols : (r + 1) * cols]


def project_first(n0, n1, n2, mine, q, g, k, v):
    project_queries(n0, mine, q, g)
    project_keys((n0, n1, n2), mine, k, v)


def project_second(n0, n1, n2, n3, mine, other, q, g, k, v, k_late, v_late):
    project_queries(n0, other, q, g)
    project_keys((n0, n1, n2, n3), other, k, v)
    project_keys((n3,), mine, k_late, v_late)


def attend_kernel(scalars, counts, q_ref, g_ref, *rest, phase, groups):
    parts = 2 - phase
    k_refs, v_refs, rest = rest[:parts], rest[parts : 2 * parts], rest[2 * parts :]
    b0, b1, *rest = rest
    if phase == 0:
        out_ref, bias_scr, s0, s1, t0, t1, done_scr = rest
    else:
        before_ref, wout_ref, keep_ref, send_ref, bias_scr, s0, s1, t0, t1, done_scr = rest
    step = pl.program_id(0)
    place, lane_at, seq, core = scalars[0], scalars[1], scalars[2], scalars[3]
    rows, cols, channels = q_ref.shape
    length = cols * groups
    block = cols // SEGMENT
    offsets = (0, groups - 1, 1, 2)

    @pl.when(step == 0)
    def _():
        for ref, ds in ((b0, (0, 5, 3)), (b1, (7, 4, 2, 1, 6))):
            for n, d in enumerate(ds):
                at = pl.multiple_of(lax.rem(place + d, SEGMENT) * block, block)
                for r in range(groups):
                    who = lax.rem(lane_at + offsets[r], groups)
                    for h in range(2):
                        bias_scr[pl.ds(h * cols + at, block), r * cols : (r + 1) * cols] = (
                            ref[n, who, h].astype(jnp.float32) * LOG2E
                        )

    lanes = lax.broadcasted_iota(jnp.int32, (16, TILE), 1)
    per = cols // TILE
    lane = lax.broadcasted_iota(jnp.int32, (1, 128), 1)
    slot = lax.rem(lane, 64) // HEAD_DIM
    one = jnp.where(lane == 0, 1.0, 0.0).astype(jnp.bfloat16)
    flag = jnp.broadcast_to(one, (2 * cols, 128))[:, :16]
    zero = jnp.zeros((cols, 128), jnp.bfloat16)

    def score(i, s_ref, t_ref):
        hide = []
        for r in range(groups):
            who = lax.rem(lane_at + offsets[r], groups)
            for t in range(per):
                tile = who * per + t
                count = counts[(step * rows + i) * (groups * per) + tile]
                limit = jnp.minimum(count, seq - tile * TILE)
                hide.append(jnp.where(lanes < limit, 0.0, MASKED))
        hide = jnp.concatenate(hide, axis=1).astype(jnp.bfloat16)
        k = jnp.concatenate([ref[i] for ref in k_refs], axis=1)
        right = jnp.concatenate([k, k, hide], axis=0)
        q = q_ref[i]
        left = jnp.concatenate([jnp.where(slot == h, q, zero) for h in range(2)], axis=0)
        left = jnp.concatenate([left, flag], axis=1)
        for c in range(0, length, 256):
            s = jnp.dot(left, right[:, c : c + 256], preferred_element_type=jnp.float32)
            s = s + bias_scr[:, c : c + 256]
            s_ref[:, c : c + 256] = s
            m = jnp.maximum(s[:, :128], s[:, 128:])
            t_ref[...] = m if c == 0 else jnp.maximum(t_ref[...], m)
        top = jnp.maximum(jnp.max(t_ref[...], axis=1, keepdims=True), FLOOR)
        t_ref[...] = jnp.broadcast_to(top, t_ref.shape)

    def mix(i, s_ref, t_ref):
        v = jnp.concatenate([ref[i] for ref in v_refs], axis=0)
        values = jnp.concatenate([v, jnp.ones_like(v)], axis=1)
        p = jnp.concatenate(
            [
                jnp.exp2(s_ref[:, c : c + 128] - t_ref[...]).astype(jnp.bfloat16)
                for c in range(0, length, 128)
            ],
            axis=1,
        )
        o = jnp.dot(p, values, preferred_element_type=jnp.float32)
        a = o[:, :128] / jnp.maximum(o[:, 128:], 1.0)
        first = lane // HEAD_DIM == 0
        second = lane // HEAD_DIM == 1
        att = jnp.where(first, a[:cols], jnp.where(second, a[cols:], 0.0))
        att = att.astype(jnp.bfloat16).astype(jnp.float32)
        gated = (g_ref[i] * att).astype(jnp.bfloat16)
        if phase == 0:
            out_ref[i] = gated
        else:
            done_scr[i * cols : (i + 1) * cols] = gated

    if phase == 1:
        wouts = []
        for c in (core, 1 - core):
            part = wout_ref[pl.ds(pl.multiple_of(c * 64, 64), 64), :]
            wouts.append(jnp.concatenate([part, jnp.zeros_like(part)], axis=0))
    bufs = ((s0, t0), (s1, t1))
    score(0, *bufs[0])
    for i in range(rows):
        if i + 1 < rows:
            score(i + 1, *bufs[(i + 1) % 2])
        mix(i, *bufs[i % 2])
    if phase == 1:
        before = before_ref[...].reshape(rows * cols, channels)
        update = jnp.dot(before, wouts[0], preferred_element_type=jnp.float32)
        update += jnp.dot(done_scr[...], wouts[1], preferred_element_type=jnp.float32)
        update = update.astype(jnp.bfloat16).reshape(q_ref.shape)
        span = cols // 2
        left, right = update[:, :span], update[:, span:]
        keep_ref[...] = jnp.where(core == 0, left, right)
        send_ref[...] = jnp.where(core == 0, right, left)


def full(shape):
    return pl.BlockSpec(shape, lambda *_: (0,) * len(shape))


def some(rows, shape):
    return pl.BlockSpec((rows, *shape), lambda i, *_: (i,) + (0,) * len(shape))


def params(mib):
    return pltpu.CompilerParams(vmem_limit_bytes=mib * 1024 * 1024)


def norm(pair, gain, w_bias, core):
    rows, cols, channels = pair.shape
    half = rows // 2
    return pl.pallas_call(
        norm_kernel,
        grid_spec=pltpu.PrefetchScalarGridSpec(
            num_scalar_prefetch=1,
            grid=(2,),
            in_specs=[
                pl.BlockSpec((half, cols, channels), lambda i, s: (lax.rem(i + s[0], 2), 0, 0)),
                full((1, channels)),
                full((2, channels)),
            ],
            out_specs=[
                full((half, cols, channels)),
                pl.BlockSpec((2, half, cols), lambda i, s: (0, lax.rem(i + s[0], 2), 0)),
            ],
            scratch_shapes=[pltpu.VMEM((2, half, cols), jnp.float32)],
        ),
        out_shape=[
            jax.ShapeDtypeStruct((half, cols, channels), jnp.bfloat16),
            jax.ShapeDtypeStruct((2, rows, cols), jnp.bfloat16),
        ],
        compiler_params=params(NORM_VMEM),
        cost_estimate=pl.CostEstimate(
            flops=4_000_000_000, bytes_accessed=4_000_000, transcendentals=0
        ),
        name="norm",
    )(core[None], pair, gain[None], w_bias.T)


def project(sources, packs):
    half, cols, channels = sources[0].shape
    step = STEP
    second = len(packs) == 2
    row = some(step, (cols, channels))
    shape = jax.ShapeDtypeStruct
    out_specs = [row, row]
    out_shape = [
        shape((half, cols, channels), jnp.bfloat16),
        shape((half, cols, channels), jnp.float32),
    ]
    for blocks in (len(sources), 1) if second else (len(sources),):
        length = blocks * cols
        out_specs += [some(step, (64, length)), some(step, (length, channels))]
        out_shape += [
            shape((half, 64, length), jnp.bfloat16),
            shape((half, length, channels), jnp.bfloat16),
        ]
    return pl.pallas_call(
        project_second if second else project_first,
        grid=(half // step,),
        in_specs=[row] * len(sources) + [full(p.shape) for p in packs],
        out_specs=out_specs,
        out_shape=out_shape,
        compiler_params=params(PROJECT_VMEM),
        cost_estimate=pl.CostEstimate(
            flops=4_000_000_000, bytes_accessed=10_000_000, transcendentals=0
        ),
    )(*sources, *packs)


def attend(scalars, counts, q, g, ks, vs, blocks, phase, groups, before=None, wout=None):
    half, cols, channels = q.shape
    length = groups * cols
    step = STEP
    row = some(step, (cols, channels))
    in_specs = [row, row]
    in_specs += [some(step, a.shape[1:]) for a in (*ks, *vs)]
    in_specs += [full(b.shape) for b in blocks]
    args = [q, g, *ks, *vs, *blocks]
    if phase == 0:
        out_specs = row
        out_shape = jax.ShapeDtypeStruct((half, cols, channels), jnp.bfloat16)
    else:
        in_specs += [row, full(wout.shape)]
        args += [before, wout]
        out_specs = [some(step, (cols // 2, channels))] * 2
        out_shape = [jax.ShapeDtypeStruct((half, cols // 2, channels), jnp.bfloat16)] * 2
    return pl.pallas_call(
        functools.partial(attend_kernel, phase=phase, groups=groups),
        grid_spec=pltpu.PrefetchScalarGridSpec(
            num_scalar_prefetch=2,
            grid=(half // step,),
            in_specs=in_specs,
            out_specs=out_specs,
            scratch_shapes=[
                pltpu.VMEM((2 * cols, length), jnp.float32),
                pltpu.VMEM((2 * cols, length), jnp.float32),
                pltpu.VMEM((2 * cols, length), jnp.float32),
                pltpu.VMEM((2 * cols, 128), jnp.float32),
                pltpu.VMEM((2 * cols, 128), jnp.float32),
                pltpu.VMEM((step * cols, channels), jnp.bfloat16),
            ],
        ),
        out_shape=out_shape,
        compiler_params=params(ATTEND_VMEM),
        cost_estimate=pl.CostEstimate(
            flops=14_000_000_000, bytes_accessed=16_000_000, transcendentals=8_000_000
        ),
    )(scalars, counts, *args)


def per_device(
    pair, seq_length, tile_counts, ln_gain, w_query, w_key, w_value, w_gate, w_bias, w_out
):
    rows, _, _ = pair.shape
    half = rows // 2
    size = lax.axis_size("rows")
    groups = lax.axis_size("keys")
    core = lax.axis_index("heads")
    place = lax.rem(lax.axis_index("rows"), SEGMENT)
    lane_at = lax.axis_index("keys")
    swap = [(0, 1), (1, 0)]

    n0, bias = norm(pair, ln_gain, w_bias, core)

    n1 = lax.ppermute(n0, "keys", shift(groups, 1))
    n2 = lax.ppermute(n0, "keys", shift(groups, -1))

    stride = [[i + SEGMENT * j for j in range(size // SEGMENT)] for i in range(SEGMENT)]
    far = lax.all_gather(bias, "rows", axis=0, axis_index_groups=stride)
    turned = lax.all_to_all(far, "keys", 0, 0, tiled=True)
    down = lax.ppermute(turned, "rows", shift(size, 3))
    up = lax.ppermute(turned, "rows", shift(size, -3))

    blank = jnp.zeros_like(w_query)
    turned_key = jnp.concatenate([w_key.T, blank.T], axis=0)
    mine = jnp.concatenate(
        [w_query, w_query, w_gate, blank, w_value, blank, turned_key], axis=1
    )
    mine, _ = lax.optimization_barrier((mine, far))
    other = lax.ppermute(mine, "heads", swap)
    late, _ = lax.optimization_barrier((n0, far))
    n3 = lax.ppermute(late, "keys", shift(groups, 2))

    q0, g0, k0, v0 = project((n0, n1, n2), (mine,))
    down, up, q0 = lax.optimization_barrier((down, up, q0))

    three = jnp.stack([turned, down, up])
    below = lax.ppermute(three, "rows", shift(size, 1))
    above = lax.ppermute(three[:2], "rows", shift(size, -1))
    other, _ = lax.optimization_barrier((other, q0))
    q1, g1, k1, v1, k_late, v_late = project((n0, n1, n2, n3), (mine, other))
    below, above, q1 = lax.optimization_barrier((below, above, q1))
    five = jnp.concatenate([below, above])

    blocks = (three, five)
    three_other = lax.ppermute(three, "heads", swap)
    blocks_other = (three_other, lax.ppermute(five, "heads", swap))

    scalars = jnp.stack([place, lane_at, seq_length[0], core]).astype(jnp.int32)
    counts = lax.dynamic_slice_in_dim(tile_counts, core * half, half, 0).reshape(-1)
    gated = attend(
        scalars, counts, q0, g0, (k0, k_late), (v0, v_late), blocks, 0, groups
    )
    keep, send = attend(
        scalars, counts, q1, g1, (k1,), (v1,), blocks_other, 1, groups, gated, w_out
    )

    got = lax.ppermute(send, "heads", swap)
    return jnp.where(
        core == 0, jnp.concatenate([keep, got], axis=0), jnp.concatenate([got, keep], axis=0)
    )


def solution(mesh):
    in_specs = (
        P(("groups", "rows"), "keys", None),
        P("groups"),
        P(("groups", "rows"), None),
        P(),
        P(None, "heads"),
        P(None, "heads"),
        P(None, "heads"),
        P(None, "heads"),
        P(None, "heads"),
        P(),
    )
    out_specs = P(("groups", "rows"), ("keys", "heads"), None)

    return jax.shard_map(per_device, mesh=mesh, in_specs=in_specs, out_specs=out_specs, check_vma=False)
```

profile of v0, /device:TPU:33, one launch (start us, length us, event | category | flops | bytes accessed | tf_op | source)
XLA Modules:
  0.0 176.1 jit_solution(6098232463827285186)
XLA Ops:
  0.0 1.6 copy-done.1
  2.9 3.5 %norm.1 = (bf16[16,256,128]{2,1,0:T(8,128)(2,1)S(1)}, bf16[2,32,256]{2,1,0:T(8,128)(2,1)S(1)}) custom-call(s32[1]{0:T(128)} %bitcast.2.scalars, bf16[32,256,128]{2,1,0:T(8,128)(2,1)S(1)} %copy-done.1, f32[1,128]{1,0:T(1,128)S(1)} %bitcast.10, bf16[2,128]{1,0:T(2,128)(2,1)S(1)} %bitcast.11), custom_call_target="tpu_custom_call" | custom-call | flops 4000000000 | bytes 4000000 | tf_op jit(solution)/shard_map/norm/pallas_call | solution.py:209
  6.4 4.1 %collective-permute-start.2 = (bf16[16,256,128]{2,1,0:T(8,128)(2,1)S(1)}, bf16[16,256,128]{2,1,0:T(8,128)(2,1)S(1)}, u32[]{:S(2)}, u32[]{:S(2)}) collective-permute-start(bf16[16,256,128]{2,1,0:T(8,128)(2,1)S(1)} %get-tuple-element.34.n0), channel_id=1, source_target_pairs={{0,2},{2,4},{4,6},{6,0},{1,3},{3,5},{5,7},{7,1},{8,10},{10,12},{12... | collective-permute-start | bytes 3145736 | tf_op jit(solution)/shard_map/ppermute | solution.py:323
  10.5 3.5 %collective-permute-start.3 = (bf16[16,256,128]{2,1,0:T(8,128)(2,1)S(1)}, bf16[16,256,128]{2,1,0:T(8,128)(2,1)}, u32[]{:S(2)}, u32[]{:S(2)}) collective-permute-start(bf16[16,256,128]{2,1,0:T(8,128)(2,1)S(1)} %get-tuple-element.34.n0), channel_id=1, source_target_pairs={{0,6},{2,0},{4,2},{6,4},{1,7},{3,1},{5,3},{7,5},{8,14},{10,8},{12,... | collective-permute-start | bytes 3145736 | tf_op jit(solution)/shard_map/ppermute | solution.py:324
  14.0 60.8 %all-gather = bf16[8,32,256]{2,1,0:T(8,128)(2,1)} all-gather(bf16[2,32,256]{2,1,0:T(8,128)(2,1)S(1)} %get-tuple-element.28), channel_id=2, replica_groups={{0,64,128,192},{8,72,136,200},{16,80,144,208},{24,88,152,216},{32,96,16..., dimensions={0}, use_global_device_ids=true | all-gather | bytes 163840 | tf_op jit(solution)/shard_map/all_gather | solution.py:327
  74.8 2.7 %collective-permute-start.6 = (bf16[16,256,128]{2,1,0:T(8,128)(2,1)S(1)}, bf16[16,256,128]{2,1,0:T(8,128)(2,1)}, u32[]{:S(2)}, u32[]{:S(2)}) collective-permute-start(bf16[16,256,128]{2,1,0:T(8,128)(2,1)S(1)} %get-tuple-element.34.n0), channel_id=1, source_target_pairs={{0,4},{2,6},{4,0},{6,2},{1,5},{3,7},{5,1},{7,3},{8,12},{10,14},{12... | collective-permute-start | bytes 3145736 | tf_op jit(solution)/shard_map/ppermute | solution.py:340
  77.6 3.5 %all-to-all-start = ((bf16[4,2,32,256]{3,2,1,0:T(8,128)(2,1)}), bf16[4,2,32,256]{3,2,1,0:T(8,128)(2,1)S(1)}, u32[]{:S(2)}, u32[]{:S(2)}) async-start(bf16[4,2,32,256]{3,2,1,0:T(8,128)(2,1)} %bitcast.5), calls=%async_computation | async-start | bytes 262144 | tf_op jit(solution)/shard_map/all_to_all | solution.py:328
  81.6 11.6 %collective-permute-start.7 = (bf16[128,512]{1,0:T(8,128)(2,1)S(1)}, bf16[128,512]{1,0:T(8,128)(2,1)S(1)}, u32[]{:S(2)}, u32[]{:S(2)}) collective-permute-start(bf16[128,512]{1,0:T(8,128)(2,1)S(1)} %concatenate.17.mine), channel_id=1, source_target_pairs={{0,1},{1,0},{2,3},{3,2},{4,5},{5,4},{6,7},{7,6},{8,9},{9,8},{10,11... | collective-permute-start | bytes 393224 | tf_op jit(solution)/shard_map/ppermute | solution.py:338
  94.2 1.2 all-to-all-done
  95.4 14.4 %collective-permute-start = (bf16[4,2,32,256]{3,2,1,0:T(8,128)(2,1)S(1)}, bf16[4,2,32,256]{3,2,1,0:T(8,128)(2,1)S(1)}, u32[]{:S(2)}, u32[]{:S(2)}) collective-permute-start(bf16[4,2,32,256]{3,2,1,0:T(8,128)(2,1)S(1)} %all-to-all-done), channel_id=1, source_target_pairs={{0,24},{8,32},{16,40},{24,48},{32,56},{40,64},{48,72},{56,80},{64,... | collective-permute-start | bytes 393224 | tf_op jit(solution)/shard_map/ppermute | solution.py:329
  109.9 5.7 %collective-permute-start.1 = (bf16[4,2,32,256]{3,2,1,0:T(8,128)(2,1)S(1)}, bf16[4,2,32,256]{3,2,1,0:T(8,128)(2,1)S(1)}, u32[]{:S(2)}, u32[]{:S(2)}) collective-permute-start(bf16[4,2,32,256]{3,2,1,0:T(8,128)(2,1)S(1)} %all-to-all-done), channel_id=1, source_target_pairs={{0,232},{8,240},{16,248},{24,0},{32,8},{40,16},{48,24},{56,32},{64... | collective-permute-start | bytes 393224 | tf_op jit(solution)/shard_map/ppermute | solution.py:330
  115.6 3.7 %shard_map.100 = (bf16[16,256,128]{2,1,0:T(8,128)(2,1)S(1)}, f32[16,256,128]{2,1,0:T(8,128)S(1)}, bf16[16,64,768]{2,1,0:T(8,128)(2,1)S(1)}, bf16[16,768,128]{2,1,0:T(8,128)(2,1)S(1)}) custom-call(bf16[16,256,128]{2,1,0:T(8,128)(2,1)S(1)} %get-tuple-element.34.n0, bf16[16,256,128]{2,1,0:T(8,128)(2,1)S(1)} %collective-permute-done.2.n1, ...), custom_call_target="tpu_custom_call" | custom-call | flops 4000000000 | bytes 10000000 | tf_op jit(solution)/shard_map/pallas_call | solution.py:255
  119.3 0.9 collective-permute-done.1
  120.3 6.1 %collective-permute-start.4 = (bf16[3,4,2,32,256]{4,3,2,1,0:T(8,128)(2,1)S(1)}, bf16[3,4,2,32,256]{4,3,2,1,0:T(8,128)(2,1)S(1)}, u32[]{:S(2)}, u32[]{:S(2)}) collective-permute-start(bf16[3,4,2,32,256]{4,3,2,1,0:T(8,128)(2,1)S(1)} %pad_maximum_fusion.rest_4_), channel_id=1, source_target_pairs={{0,8},{8,16},{16,24},{24,32},{32,40},{40,48},{48,56},{56,64},{64,7... | collective-permute-start | bytes 1179656 | tf_op jit(solution)/shard_map/ppermute | solution.py:346
  126.4 6.6 %collective-permute-start.8 = (bf16[3,4,2,32,256]{4,3,2,1,0:T(8,128)(2,1)S(1)}, bf16[3,4,2,32,256]{4,3,2,1,0:T(8,128)(2,1)S(1)}, u32[]{:S(2)}, u32[]{:S(2)}) collective-permute-start(bf16[3,4,2,32,256]{4,3,2,1,0:T(8,128)(2,1)S(1)} %pad_maximum_fusion.rest_4_), channel_id=1, source_target_pairs={{0,1},{1,0},{2,3},{3,2},{4,5},{5,4},{6,7},{7,6},{8,9},{9,8},{10,11... | collective-permute-start | bytes 1179656 | tf_op jit(solution)/shard_map/ppermute | solution.py:354
  133.0 2.9 %collective-permute-start.5 = (bf16[2,4,2,32,256]{4,3,2,1,0:T(8,128)(2,1)S(1)}, bf16[2,4,2,32,256]{4,3,2,1,0:T(8,128)(2,1)S(1)}, u32[]{:S(2)}, u32[]{:S(2)}) collective-permute-start(bf16[2,4,2,32,256]{4,3,2,1,0:T(8,128)(2,1)S(1)} %pad_maximum_fusion.1), channel_id=1, source_target_pairs={{0,248},{8,0},{16,8},{24,16},{32,24},{40,32},{48,40},{56,48},{64,5... | collective-permute-start | bytes 786440 | tf_op jit(solution)/shard_map/ppermute | solution.py:347
  135.9 5.2 %shard_map.101 = (bf16[16,256,128]{2,1,0:T(8,128)(2,1)S(1)}, f32[16,256,128]{2,1,0:T(8,128)S(1)}, bf16[16,64,1024]{2,1,0:T(8,128)(2,1)S(1)}, bf16[16,1024,128]{2...) custom-call(bf16[16,256,128]{2,1,0:T(8,128)(2,1)S(1)} %get-tuple-element.34.n0, ...), custom_call_target="tpu_custom_call" | custom-call | flops 4000000000 | bytes 10000000 | tf_op jit(solution)/shard_map/pallas_call | solution.py:255
  141.1 1.7 collective-permute-done.5
  142.8 3.0 %collective-permute-start.9 = (bf16[5,4,2,32,256]{4,3,2,1,0:T(8,128)(2,1)S(1)}, bf16[5,4,2,32,256]{4,3,2,1,0:T(8,128)(2,1)S(1)}, u32[]{:S(2)}, u32[]{:S(2)}) collective-permute-start(bf16[5,4,2,32,256]{4,3,2,1,0:T(8,128)(2,1)S(1)} %constant_dynamic-update-slice_fusion.rest_5_), channel_id=1, source_target_pairs={{0,1},{1,0},{2,3},{3,2},{4,5},{5,4},{6,7},{7,6},{8,9},{9,8},{10,11... | collective-permute-start | bytes 1966088 | tf_op jit(solution)/shard_map/ppermute | solution.py:355
  145.8 12.2 %shard_map.102.rest_4_ = bf16[16,256,128]{2,1,0:T(8,128)(2,1)S(1)} custom-call(s32[4]{0:T(128)S(1)} %pad_add_fusion.scalars, s32[128]{0:T(128)S(1)} %reshape.3.counts, bf16[16,256,128]{2,1,0:T(8,128)(2,1)S(1)} %get-tuple-element.35.q_ref, f32[16,256,128]{2,1,0:T(8,128)S(1)} %get-tuple-element.44.g_ref, bf16[16,64,768]{2,1,0:T(8,128)(2,1)S(1)} %get-tuple-element.45.rest_0_, ...), custom_call_target="tpu_custom_call" | custom-call | flops 14000000000 | bytes 16000000 | tf_op jit(solution)/shard_map/pallas_call | solution.py:285
  158.1 13.1 %shard_map.103 = (bf16[16,128,128]{2,1,0:T(8,128)(2,1)S(1)}, bf16[16,128,128]{2,1,0:T(8,128)(2,1)S(1)}) custom-call(s32[4]{0:T(128)S(1)} %pad_add_fusion.scalars, s32[128]{0:T(128)S(1)} %reshape.3.counts, bf16[16,256,128]{2,1,0:T(8,128)(2,1)S(1)} %get-tuple-element.38.q_ref, f32[16,256,128]{2,1,0:T(8,128)S(1)} %get-tuple-element.39.g_ref, ...), custom_call_target="tpu_custom_call" | custom-call | flops 14000000000 | bytes 16000000 | tf_op jit(solution)/shard_map/pallas_call | solution.py:285
  171.2 2.0 %collective-permute-start.10 = (bf16[16,128,128]{2,1,0:T(8,128)(2,1)S(1)}, bf16[16,128,128]{2,1,0:T(8,128)(2,1)S(1)}, u32[]{:S(2)}, u32[]{:S(2)}) collective-permute-start(bf16[16,128,128]{2,1,0:T(8,128)(2,1)S(1)} %get-tuple-element.50), channel_id=1, source_target_pairs={{0,1},{1,0},{2,3},{3,2},{4,5},{5,4},{6,7},{7,6},{8,9},{9,8},{10,11... | collective-permute-start | bytes 1572872 | tf_op jit(solution)/shard_map/ppermute | solution.py:366
  173.1 1.9 %collective-permute-done.10 = bf16[16,128,128]{2,1,0:T(8,128)(2,1)S(1)} collective-permute-done((bf16[16,128,128]{2,1,0:T(8,128)(2,1)S(1)}, bf16[16,128,128]{2,1,0:T(8,128)(2,1)S(1)}, u32[]{:S(2)}, u32[]{:S(2)}) %collective-permute-start.10) | collective-permute-done | bytes 524320 | tf_op jit(solution)/shard_map/ppermute | solution.py:366
  175.0 1.1 maximum_select_fusion
  (39 shorter events, 2.3 us)
Async XLA Ops:
  0.0 93.9 %copy-start = (s32[32,8]{0,1:T(8,128)S(1)}, s32[32,8]{0,1:T(8,128)}, u32[]{:S(2)}) copy-start(s32[32,8]{0,1:T(8,128)} %param.12) | copy-start | bytes 3076
  0.0 1.6 copy-start.1
  1.6 0.7 copy-start.3
  2.3 0.7 copy-start.4
  2.9 78.1 %copy-start.5 = (bf16[128,64]{0,1:T(8,128)(2,1)S(1)}, bf16[128,64]{0,1:T(8,128)(2,1)}, u32[]{:S(2)}) copy-start(bf16[128,64]{0,1:T(8,128)(2,1)} %param.14) | copy-start | bytes 49156
  2.9 78.2 %copy-start.6 = (bf16[128,64]{0,1:T(8,128)(2,1)S(1)}, bf16[128,64]{0,1:T(8,128)(2,1)}, u32[]{:S(2)}) copy-start(bf16[128,64]{0,1:T(8,128)(2,1)} %param.17) | copy-start | bytes 49156
  2.9 78.4 %copy-start.7 = (bf16[128,64]{0,1:T(8,128)(2,1)S(1)}, bf16[128,64]{0,1:T(8,128)(2,1)}, u32[]{:S(2)}) copy-start(bf16[128,64]{0,1:T(8,128)(2,1)} %param.16) | copy-start | bytes 49156
  2.9 78.5 %copy-start.8 = (bf16[128,64]{0,1:T(8,128)(2,1)S(1)}, bf16[128,64]{0,1:T(8,128)(2,1)}, u32[]{:S(2)}) copy-start(bf16[128,64]{0,1:T(8,128)(2,1)} %param.15) | copy-start | bytes 49156
  6.4 103.5 %collective-permute-start.2 = (bf16[16,256,128]{2,1,0:T(8,128)(2,1)S(1)}, bf16[16,256,128]{2,1,0:T(8,128)(2,1)S(1)}, u32[]{:S(2)}, u32[]{:S(2)}) collective-permute-start(bf16[16,256,128]{2,1,0:T(8,128)(2,1)S(1)} %get-tuple-element.34.n0), channel_id=1, source_target_pairs={{0,2},{2,4},{4,6},{6,0},{1,3},{3,5},{5,7},{7,1},{8,10},{10,12},{12... | collective-permute-start | bytes 3145736 | tf_op jit(solution)/shard_map/ppermute | solution.py:323
  10.5 105.0 %collective-permute-start.3 = (bf16[16,256,128]{2,1,0:T(8,128)(2,1)S(1)}, bf16[16,256,128]{2,1,0:T(8,128)(2,1)}, u32[]{:S(2)}, u32[]{:S(2)}) collective-permute-start(bf16[16,256,128]{2,1,0:T(8,128)(2,1)S(1)} %get-tuple-element.34.n0), channel_id=1, source_target_pairs={{0,6},{2,0},{4,2},{6,4},{1,7},{3,1},{5,3},{7,5},{8,14},{10,8},{12,... | collective-permute-start | bytes 3145736 | tf_op jit(solution)/shard_map/ppermute | solution.py:324
  74.8 61.1 %collective-permute-start.6 = (bf16[16,256,128]{2,1,0:T(8,128)(2,1)S(1)}, bf16[16,256,128]{2,1,0:T(8,128)(2,1)}, u32[]{:S(2)}, u32[]{:S(2)}) collective-permute-start(bf16[16,256,128]{2,1,0:T(8,128)(2,1)S(1)} %get-tuple-element.34.n0), channel_id=1, source_target_pairs={{0,4},{2,6},{4,0},{6,2},{1,5},{3,7},{5,1},{7,3},{8,12},{10,14},{12... | collective-permute-start | bytes 3145736 | tf_op jit(solution)/shard_map/ppermute | solution.py:340
  77.6 17.9 %all-to-all-start = ((bf16[4,2,32,256]{3,2,1,0:T(8,128)(2,1)}), bf16[4,2,32,256]{3,2,1,0:T(8,128)(2,1)S(1)}, u32[]{:S(2)}, u32[]{:S(2)}) async-start(bf16[4,2,32,256]{3,2,1,0:T(8,128)(2,1)} %bitcast.5), calls=%async_computation | async-start | bytes 262144 | tf_op jit(solution)/shard_map/all_to_all | solution.py:328
  81.6 51.4 %collective-permute-start.7 = (bf16[128,512]{1,0:T(8,128)(2,1)S(1)}, bf16[128,512]{1,0:T(8,128)(2,1)S(1)}, u32[]{:S(2)}, u32[]{:S(2)}) collective-permute-start(bf16[128,512]{1,0:T(8,128)(2,1)S(1)} %concatenate.17.mine), channel_id=1, source_target_pairs={{0,1},{1,0},{2,3},{3,2},{4,5},{5,4},{6,7},{7,6},{8,9},{9,8},{10,11... | collective-permute-start | bytes 393224 | tf_op jit(solution)/shard_map/ppermute | solution.py:338
  95.4 23.9 %collective-permute-start = (bf16[4,2,32,256]{3,2,1,0:T(8,128)(2,1)S(1)}, bf16[4,2,32,256]{3,2,1,0:T(8,128)(2,1)S(1)}, u32[]{:S(2)}, u32[]{:S(2)}) collective-permute-start(bf16[4,2,32,256]{3,2,1,0:T(8,128)(2,1)S(1)} %all-to-all-done), channel_id=1, source_target_pairs={{0,24},{8,32},{16,40},{24,48},{32,56},{40,64},{48,72},{56,80},{64,... | collective-permute-start | bytes 393224 | tf_op jit(solution)/shard_map/ppermute | solution.py:329
  109.9 10.4 %collective-permute-start.1 = (bf16[4,2,32,256]{3,2,1,0:T(8,128)(2,1)S(1)}, bf16[4,2,32,256]{3,2,1,0:T(8,128)(2,1)S(1)}, u32[]{:S(2)}, u32[]{:S(2)}) collective-permute-start(bf16[4,2,32,256]{3,2,1,0:T(8,128)(2,1)S(1)} %all-to-all-done), channel_id=1, source_target_pairs={{0,232},{8,240},{16,248},{24,0},{32,8},{40,16},{48,24},{56,32},{64... | collective-permute-start | bytes 393224 | tf_op jit(solution)/shard_map/ppermute | solution.py:330
  120.3 22.5 %collective-permute-start.4 = (bf16[3,4,2,32,256]{4,3,2,1,0:T(8,128)(2,1)S(1)}, bf16[3,4,2,32,256]{4,3,2,1,0:T(8,128)(2,1)S(1)}, u32[]{:S(2)}, u32[]{:S(2)}) collective-permute-start(bf16[3,4,2,32,256]{4,3,2,1,0:T(8,128)(2,1)S(1)} %pad_maximum_fusion.rest_4_), channel_id=1, source_target_pairs={{0,8},{8,16},{16,24},{24,32},{32,40},{40,48},{48,56},{56,64},{64,7... | collective-permute-start | bytes 1179656 | tf_op jit(solution)/shard_map/ppermute | solution.py:346
  126.4 31.6 %collective-permute-start.8 = (bf16[3,4,2,32,256]{4,3,2,1,0:T(8,128)(2,1)S(1)}, bf16[3,4,2,32,256]{4,3,2,1,0:T(8,128)(2,1)S(1)}, u32[]{:S(2)}, u32[]{:S(2)}) collective-permute-start(bf16[3,4,2,32,256]{4,3,2,1,0:T(8,128)(2,1)S(1)} %pad_maximum_fusion.rest_4_), channel_id=1, source_target_pairs={{0,1},{1,0},{2,3},{3,2},{4,5},{5,4},{6,7},{7,6},{8,9},{9,8},{10,11... | collective-permute-start | bytes 1179656 | tf_op jit(solution)/shard_map/ppermute | solution.py:354
  133.0 9.8 %collective-permute-start.5 = (bf16[2,4,2,32,256]{4,3,2,1,0:T(8,128)(2,1)S(1)}, bf16[2,4,2,32,256]{4,3,2,1,0:T(8,128)(2,1)S(1)}, u32[]{:S(2)}, u32[]{:S(2)}) collective-permute-start(bf16[2,4,2,32,256]{4,3,2,1,0:T(8,128)(2,1)S(1)} %pad_maximum_fusion.1), channel_id=1, source_target_pairs={{0,248},{8,0},{16,8},{24,16},{32,24},{40,32},{48,40},{56,48},{64,5... | collective-permute-start | bytes 786440 | tf_op jit(solution)/shard_map/ppermute | solution.py:347
  142.8 15.2 %collective-permute-start.9 = (bf16[5,4,2,32,256]{4,3,2,1,0:T(8,128)(2,1)S(1)}, bf16[5,4,2,32,256]{4,3,2,1,0:T(8,128)(2,1)S(1)}, u32[]{:S(2)}, u32[]{:S(2)}) collective-permute-start(bf16[5,4,2,32,256]{4,3,2,1,0:T(8,128)(2,1)S(1)} %constant_dynamic-update-slice_fusion.rest_5_), channel_id=1, source_target_pairs={{0,1},{1,0},{2,3},{3,2},{4,5},{5,4},{6,7},{7,6},{8,9},{9,8},{10,11... | collective-permute-start | bytes 1966088 | tf_op jit(solution)/shard_map/ppermute | solution.py:355
  145.8 12.2 %copy-start.2 = (bf16[128,128]{1,0:T(8,128)(2,1)S(1)}, bf16[128,128]{1,0:T(8,128)(2,1)}, u32[]{:S(2)}) copy-start(bf16[128,128]{1,0:T(8,128)(2,1)} %rest_5_.1) | copy-start | bytes 98308
  171.2 3.8 %collective-permute-start.10 = (bf16[16,128,128]{2,1,0:T(8,128)(2,1)S(1)}, bf16[16,128,128]{2,1,0:T(8,128)(2,1)S(1)}, u32[]{:S(2)}, u32[]{:S(2)}) collective-permute-start(bf16[16,128,128]{2,1,0:T(8,128)(2,1)S(1)} %get-tuple-element.50), channel_id=1, source_target_pairs={{0,1},{1,0},{2,3},{3,2},{4,5},{5,4},{6,7},{7,6},{8,9},{9,8},{10,11... | collective-permute-start | bytes 1572872 | tf_op jit(solution)/shard_map/ppermute | solution.py:366
where the time goes:
time: 177 us; the launch traced here: 176 us
  starting transfers between devices  66 us (37%)
  blocking collectives  60.8 us (34%)
  Pallas kernels  37.7 us (21%)
  waiting for transfers between devices  5.73 us (3%)
  local copies, waits for them, and re-layouts  3.7 us (2%)
    all_gather x1, blocking collectives, per_device(): far = lax.all_gather(bias, 'rows', axis=0, axis_index_groups=stride)  60.8 us
    pallas_call x2, Pallas kernels, attend(): pl.pallas_call(functools.partial(attend_kernel, phase=phase, groups=group...  25.3 us
    ppermute x1, starting transfers between devices, per_device(): down = lax.ppermute(turned, 'rows', shift(size, 3))  14.4 us
    ppermute x1, starting transfers between devices, per_device(): other = lax.ppermute(mine, 'heads', swap)  11.6 us
    pallas_call x2, Pallas kernels, project(): pl.pallas_call(project_second if second else project_first, grid=(half //...  8.91 us
    ppermute x1, starting transfers between devices, per_device(): three_other = lax.ppermute(three, 'heads', swap)  6.56 us
    ppermute x1, starting transfers between devices, per_device(): below = lax.ppermute(three, 'rows', shift(size, 1))  6.06 us
    ppermute x1, starting transfers between devices, per_device(): up = lax.ppermute(turned, 'rows', shift(size, -3))  5.68 us
  transfers between devices with their start and end apart: 12, of which 4 were waited for; matrix products, arithmetic and copies ran while one was open for 1% of the time, Pallas kernels for 12%

commit v1 on v0

--- a/solution.py
+++ b/solution.py
@@ -16,7 +16,7 @@
 SEGMENT = 8
 STEP = 8
 LOG2E = 1.4426950408889634
-NORM_VMEM = 20
+NORM_VMEM = 60
 PROJECT_VMEM = 20
 ATTEND_VMEM = 32
 
@@ -331,12 +331,10 @@
 
     blank = jnp.zeros_like(w_query)
     turned_key = jnp.concatenate([w_key.T, blank.T], axis=0)
-    mine = jnp.concatenate(
-        [w_query, w_query, w_gate, blank, w_value, blank, turned_key], axis=1
-    )
+    mine = jnp.concatenate([w_query, w_query, w_gate, blank, w_value, blank, turned_key], axis=1)
     mine, _ = lax.optimization_barrier((mine, far))
     other = lax.ppermute(mine, "heads", swap)
-    late, _ = lax.optimization_barrier((n0, far))
+    late, _ = lax.optimization_barrier((n0, turned))
     n3 = lax.ppermute(late, "keys", shift(groups, 2))
 
     q0, g0, k0, v0 = project((n0, n1, n2), (mine,))

time: 177 us -> 176 us (level)
  starting transfers between devices: 66 us -> 57.4 us
  blocking collectives: 60.8 us -> 68.2 us
    ppermute x1, starting transfers between devices: 14.4 us -> 1.94 us  [per_device(): down = lax.ppermute(turned, 'rows', shift(size, 3))]
    ppermute x1, starting transfers between devices: 11.6 us -> 21.1 us  [per_device(): other = lax.ppermute(mine, 'heads', swap)]
    all_to_all x0 -> x1, blocking collectives: none -> 7.53 us  [per_device(): turned = lax.all_to_all(far, 'keys', 0, 0, tiled=True)]
    ppermute x1, starting transfers between devices: 5.68 us -> 9.83 us  [per_device(): up = lax.ppermute(turned, 'rows', shift(size, -3))]
    ppermute x1, starting transfers between devices: 6.56 us -> 2.63 us  [per_device(): three_other = lax.ppermute(three, 'heads', swap)]
    ppermute x1, starting transfers between devices: 6.06 us -> 2.39 us  [per_device(): below = lax.ppermute(three, 'rows', shift(size, 1))]
    all_to_all x1 -> x0, starting transfers between devices: 3.48 us -> none  [per_device(): turned = lax.all_to_all(far, 'keys', 0, 0, tiled=True)]
    ppermute x1, waiting for transfers between devices: 0.92 us -> 4.35 us  [per_device(): up = lax.ppermute(turned, 'rows', shift(size, -3))]
  transfers between devices with their start and end apart: 12 -> 11, of which waited for: 4 -> 3; matrix products, arithmetic and copies ran while one was open for 1% -> 1% of each run, Pallas kernels for 12% -> 11%
where the time goes in v1:
time: 176 us; the launch traced here: 175 us
  blocking collectives  68.2 us (39%)
  starting transfers between devices  57.4 us (33%)
  Pallas kernels  38.4 us (22%)
  waiting for transfers between devices  6.85 us (4%)
  local copies, waits for them, and re-layouts  2 us (1%)
    all_gather x1, blocking collectives, per_device(): far = lax.all_gather(bias, 'rows', axis=0, axis_index_groups=stride)  60.7 us
    pallas_call x2, Pallas kernels, attend(): pl.pallas_call(functools.partial(attend_kernel, phase=phase, groups=group...  25.3 us
    ppermute x1, starting transfers between devices, per_device(): other = lax.ppermute(mine, 'heads', swap)  21.1 us
    ppermute x1, starting transfers between devices, per_device(): up = lax.ppermute(turned, 'rows', shift(size, -3))  9.83 us
    pallas_call x2, Pallas kernels, project(): pl.pallas_call(project_second if second else project_first, grid=(half //...  7.68 us
    all_to_all x1, blocking collectives, per_device(): turned = lax.all_to_all(far, 'keys', 0, 0, tiled=True)  7.53 us
    pallas_call x1, Pallas kernels, norm(): pl.pallas_call(norm_kernel, grid_spec=pltpu.PrefetchScalarGridSpec(num_sc...  5.41 us
    ppermute x1, starting transfers between devices, per_device(): above = lax.ppermute(three[:2], 'rows', shift(size, -1))  4.77 us
  transfers between devices with their start and end apart: 11, of which 3 were waited for; matrix products, arithmetic and copies ran while one was open for 1% of the time, Pallas kernels for 11%

profile of v1, /device:TPU:33, one launch (start us, length us, event | category | flops | bytes accessed | tf_op | source)
XLA Modules:
  0.0 175.2 jit_solution(3888287603095189627)
XLA Ops:
  0.0 5.4 %norm.1 = (bf16[16,256,128]{2,1,0:T(8,128)(2,1)}, bf16[2,32,256]{2,1,0:T(8,128)(2,1)}) custom-call(s32[1]{0:T(128)} %bitcast.2.scalars, bf16[32,256,128]{2,1,0:T(8,128)(2,1)} %pair_ref.1, f32[1,128]{1,0:T(1,128)} %bitcast.17, bf16[2,128]{1,0:T(2,128)(2,1)} %bitcast.18), custom_call_target="tpu_custom_call" | custom-call | flops 4000000000 | bytes 4000000 | tf_op jit(solution)/shard_map/norm/pallas_call | solution.py:209
  5.4 4.1 %collective-permute-start.2 = (bf16[16,256,128]{2,1,0:T(8,128)(2,1)}, bf16[16,256,128]{2,1,0:T(8,128)(2,1)S(1)}, u32[]{:S(2)}, u32[]{:S(2)}) collective-permute-start(bf16[16,256,128]{2,1,0:T(8,128)(2,1)} %get-tuple-element.34.n0), channel_id=1, source_target_pairs={{0,2},{2,4},{4,6},{6,0},{1,3},{3,5},{5,7},{7,1},{8,10},{10,12},{12... | collective-permute-start | bytes 3145736 | tf_op jit(solution)/shard_map/ppermute | solution.py:323
  9.5 3.5 %collective-permute-start.3 = (bf16[16,256,128]{2,1,0:T(8,128)(2,1)}, bf16[16,256,128]{2,1,0:T(8,128)(2,1)S(1)}, u32[]{:S(2)}, u32[]{:S(2)}) collective-permute-start(bf16[16,256,128]{2,1,0:T(8,128)(2,1)} %get-tuple-element.34.n0), channel_id=1, source_target_pairs={{0,6},{2,0},{4,2},{6,4},{1,7},{3,1},{5,3},{7,5},{8,14},{10,8},{12,... | collective-permute-start | bytes 3145736 | tf_op jit(solution)/shard_map/ppermute | solution.py:324
  13.0 60.7 %all-gather = bf16[8,32,256]{2,1,0:T(8,128)(2,1)S(1)} all-gather(bf16[2,32,256]{2,1,0:T(8,128)(2,1)} %get-tuple-element.28), channel_id=2, replica_groups={{0,64,128,192},{8,72,136,200},{16,80,144,208},{24,88,152,216},{32,96,16..., dimensions={0}, use_global_device_ids=true | all-gather | bytes 163840 | tf_op jit(solution)/shard_map/all_gather | solution.py:327
  73.8 7.5 %all_to_all.5 = bf16[4,2,32,256]{3,2,1,0:T(8,128)(2,1)S(1)} all-to-all(bf16[4,2,32,256]{3,2,1,0:T(8,128)(2,1)S(1)} %bitcast.12), channel_id=1, replica_groups=mesh['groups'=2,'rows'=32,'keys'=4,'heads'=2] {'keys'}, dimensions={0} | all-to-all | bytes 262144 | tf_op jit(solution)/shard_map/all_to_all | solution.py:328
  81.3 2.2 %collective-permute-start.6 = (bf16[16,256,128]{2,1,0:T(8,128)(2,1)}, bf16[16,256,128]{2,1,0:T(8,128)(2,1)}, u32[]{:S(2)}, u32[]{:S(2)}) collective-permute-start(bf16[16,256,128]{2,1,0:T(8,128)(2,1)} %get-tuple-element.34.n0), channel_id=1, source_target_pairs={{0,4},{2,6},{4,0},{6,2},{1,5},{3,7},{5,1},{7,3},{8,12},{10,14},{12... | collective-permute-start | bytes 3145736 | tf_op jit(solution)/shard_map/ppermute | solution.py:338
  83.9 0.1 concatenate.17.mine
  84.0 21.1 %collective-permute-start.7 = (bf16[128,512]{1,0:T(8,128)(2,1)S(1)}, bf16[128,512]{1,0:T(8,128)(2,1)S(1)}, u32[]{:S(2)}, u32[]{:S(2)}) collective-permute-start(bf16[128,512]{1,0:T(8,128)(2,1)S(1)} %concatenate.17.mine), channel_id=1, source_target_pairs={{0,1},{1,0},{2,3},{3,2},{4,5},{5,4},{6,7},{7,6},{8,9},{9,8},{10,11... | collective-permute-start | bytes 393224 | tf_op jit(solution)/shard_map/ppermute | solution.py:336
  106.2 1.9 %collective-permute-start = (bf16[4,2,32,256]{3,2,1,0:T(8,128)(2,1)S(1)}, bf16[4,2,32,256]{3,2,1,0:T(8,128)(2,1)S(1)}, u32[]{:S(2)}, u32[]{:S(2)}) collective-permute-start(bf16[4,2,32,256]{3,2,1,0:T(8,128)(2,1)S(1)} %all_to_all.5), channel_id=1, source_target_pairs={{0,24},{8,32},{16,40},{24,48},{32,56},{40,64},{48,72},{56,80},{64,... | collective-permute-start | bytes 393224 | tf_op jit(solution)/shard_map/ppermute | solution.py:329
  108.1 9.8 %collective-permute-start.1 = (bf16[4,2,32,256]{3,2,1,0:T(8,128)(2,1)S(1)}, bf16[4,2,32,256]{3,2,1,0:T(8,128)(2,1)S(1)}, u32[]{:S(2)}, u32[]{:S(2)}) collective-permute-start(bf16[4,2,32,256]{3,2,1,0:T(8,128)(2,1)S(1)} %all_to_all.5), channel_id=1, source_target_pairs={{0,232},{8,240},{16,248},{24,0},{32,8},{40,16},{48,24},{56,32},{64... | collective-permute-start | bytes 393224 | tf_op jit(solution)/shard_map/ppermute | solution.py:330
  118.0 1.2 copy-done.1
  119.2 2.7 %shard_map.100 = (bf16[16,256,128]{2,1,0:T(8,128)(2,1)S(1)}, f32[16,256,128]{2,1,0:T(8,128)S(1)}, bf16[16,64,768]{2,1,0:T(8,128)(2,1)S(1)}, bf16[16,768,128]{2,1,0:T(8,128)(2,1)S(1)}) custom-call(bf16[16,256,128]{2,1,0:T(8,128)(2,1)S(1)} %copy-done.1, bf16[16,256,128]{2,1,0:T(8,128)(2,1)S(1)} %collective-permute-done.2.n1, ...), custom_call_target="tpu_custom_call" | custom-call | flops 4000000000 | bytes 10000000 | tf_op jit(solution)/shard_map/pallas_call | solution.py:255
  121.9 4.3 %collective-permute-done.1 = bf16[4,2,32,256]{3,2,1,0:T(8,128)(2,1)S(1)} collective-permute-done((bf16[4,2,32,256]{3,2,1,0:T(8,128)(2,1)S(1)}, bf16[4,2,32,256]{3,2,1,0:T(8,128)(2,1)S(1)}, u32[]{:S(2)}, u32[]{:S(2)}) %collective-permute-start.1) | collective-permute-done | bytes 131104 | tf_op jit(solution)/shard_map/ppermute | solution.py:330
  126.3 2.4 %collective-permute-start.4 = (bf16[3,4,2,32,256]{4,3,2,1,0:T(8,128)(2,1)S(1)}, bf16[3,4,2,32,256]{4,3,2,1,0:T(8,128)(2,1)S(1)}, u32[]{:S(2)}, u32[]{:S(2)}) collective-permute-start(bf16[3,4,2,32,256]{4,3,2,1,0:T(8,128)(2,1)S(1)} %pad_maximum_fusion.rest_4_), channel_id=1, source_target_pairs={{0,8},{8,16},{16,24},{24,32},{32,40},{40,48},{48,56},{56,64},{64,7... | collective-permute-start | bytes 1179656 | tf_op jit(solution)/shard_map/ppermute | solution.py:344
  128.7 2.6 %collective-permute-start.8 = (bf16[3,4,2,32,256]{4,3,2,1,0:T(8,128)(2,1)S(1)}, bf16[3,4,2,32,256]{4,3,2,1,0:T(8,128)(2,1)S(1)}, u32[]{:S(2)}, u32[]{:S(2)}) collective-permute-start(bf16[3,4,2,32,256]{4,3,2,1,0:T(8,128)(2,1)S(1)} %pad_maximum_fusion.rest_4_), channel_id=1, source_target_pairs={{0,1},{1,0},{2,3},{3,2},{4,5},{5,4},{6,7},{7,6},{8,9},{9,8},{10,11... | collective-permute-start | bytes 1179656 | tf_op jit(solution)/shard_map/ppermute | solution.py:352
  131.4 4.8 %collective-permute-start.5 = (bf16[2,4,2,32,256]{4,3,2,1,0:T(8,128)(2,1)S(1)}, bf16[2,4,2,32,256]{4,3,2,1,0:T(8,128)(2,1)S(1)}, u32[]{:S(2)}, u32[]{:S(2)}) collective-permute-start(bf16[2,4,2,32,256]{4,3,2,1,0:T(8,128)(2,1)S(1)} %pad_maximum_fusion.1), channel_id=1, source_target_pairs={{0,248},{8,0},{16,8},{24,16},{32,24},{40,32},{48,40},{56,48},{64,5... | collective-permute-start | bytes 786440 | tf_op jit(solution)/shard_map/ppermute | solution.py:345
  136.2 5.0 %shard_map.101 = (bf16[16,256,128]{2,1,0:T(8,128)(2,1)S(1)}, f32[16,256,128]{2,1,0:T(8,128)S(1)}, bf16[16,64,1024]{2,1,0:T(8,128)(2,1)S(1)}, bf16[16,1024,128]{2...) custom-call(bf16[16,256,128]{2,1,0:T(8,128)(2,1)S(1)} %copy-done.1, ...), custom_call_target="tpu_custom_call" | custom-call | flops 4000000000 | bytes 10000000 | tf_op jit(solution)/shard_map/pallas_call | solution.py:255
  141.2 0.6 collective-permute-done.5
  141.9 3.0 %collective-permute-start.9 = (bf16[5,4,2,32,256]{4,3,2,1,0:T(8,128)(2,1)S(1)}, bf16[5,4,2,32,256]{4,3,2,1,0:T(8,128)(2,1)S(1)}, u32[]{:S(2)}, u32[]{:S(2)}) collective-permute-start(bf16[5,4,2,32,256]{4,3,2,1,0:T(8,128)(2,1)S(1)} %constant_dynamic-update-slice_fusion.rest_5_), channel_id=1, source_target_pairs={{0,1},{1,0},{2,3},{3,2},{4,5},{5,4},{6,7},{7,6},{8,9},{9,8},{10,11... | collective-permute-start | bytes 1966088 | tf_op jit(solution)/shard_map/ppermute | solution.py:353
  144.9 12.2 %shard_map.102.rest_4_ = bf16[16,256,128]{2,1,0:T(8,128)(2,1)S(1)} custom-call(s32[4]{0:T(128)S(1)} %pad_add_fusion.scalars, s32[128]{0:T(128)S(1)} %reshape.3.counts, bf16[16,256,128]{2,1,0:T(8,128)(2,1)S(1)} %get-tuple-element.35.q_ref, f32[16,256,128]{2,1,0:T(8,128)S(1)} %get-tuple-element.44.g_ref, bf16[16,64,768]{2,1,0:T(8,128)(2,1)S(1)} %get-tuple-element.45.rest_0_, ...), custom_call_target="tpu_custom_call" | custom-call | flops 14000000000 | bytes 16000000 | tf_op jit(solution)/shard_map/pallas_call | solution.py:285
  157.1 13.1 %shard_map.103 = (bf16[16,128,128]{2,1,0:T(8,128)(2,1)S(1)}, bf16[16,128,128]{2,1,0:T(8,128)(2,1)S(1)}) custom-call(s32[4]{0:T(128)S(1)} %pad_add_fusion.scalars, s32[128]{0:T(128)S(1)} %reshape.3.counts, bf16[16,256,128]{2,1,0:T(8,128)(2,1)S(1)} %get-tuple-element.38.q_ref, f32[16,256,128]{2,1,0:T(8,128)S(1)} %get-tuple-element.39.g_ref, ...), custom_call_target="tpu_custom_call" | custom-call | flops 14000000000 | bytes 16000000 | tf_op jit(solution)/shard_map/pallas_call | solution.py:285
  170.2 2.0 %collective-permute-start.10 = (bf16[16,128,128]{2,1,0:T(8,128)(2,1)S(1)}, bf16[16,128,128]{2,1,0:T(8,128)(2,1)S(1)}, u32[]{:S(2)}, u32[]{:S(2)}) collective-permute-start(bf16[16,128,128]{2,1,0:T(8,128)(2,1)S(1)} %get-tuple-element.50), channel_id=1, source_target_pairs={{0,1},{1,0},{2,3},{3,2},{4,5},{5,4},{6,7},{7,6},{8,9},{9,8},{10,11... | collective-permute-start | bytes 1572872 | tf_op jit(solution)/shard_map/ppermute | solution.py:364
  172.2 1.9 %collective-permute-done.10 = bf16[16,128,128]{2,1,0:T(8,128)(2,1)S(1)} collective-permute-done((bf16[16,128,128]{2,1,0:T(8,128)(2,1)S(1)}, bf16[16,128,128]{2,1,0:T(8,128)(2,1)S(1)}, u32[]{:S(2)}, u32[]{:S(2)}) %collective-permute-start.10) | collective-permute-done | bytes 524320 | tf_op jit(solution)/shard_map/ppermute | solution.py:364
  174.0 1.1 maximum_select_fusion
  (34 shorter events, 0.8 us)
Async XLA Ops:
  0.0 105.8 %copy-start = (s32[32,8]{0,1:T(8,128)S(1)}, s32[32,8]{0,1:T(8,128)}, u32[]{:S(2)}) copy-start(s32[32,8]{0,1:T(8,128)} %param.12) | copy-start | bytes 3076
  0.0 83.5 %copy-start.3 = (bf16[128,64]{0,1:T(8,128)(2,1)S(1)}, bf16[128,64]{0,1:T(8,128)(2,1)}, u32[]{:S(2)}) copy-start(bf16[128,64]{0,1:T(8,128)(2,1)} %param.14) | copy-start | bytes 49156
  0.0 83.6 %copy-start.4 = (bf16[128,64]{0,1:T(8,128)(2,1)S(1)}, bf16[128,64]{0,1:T(8,128)(2,1)}, u32[]{:S(2)}) copy-start(bf16[128,64]{0,1:T(8,128)(2,1)} %param.17) | copy-start | bytes 49156
  0.0 83.7 %copy-start.5 = (bf16[128,64]{0,1:T(8,128)(2,1)S(1)}, bf16[128,64]{0,1:T(8,128)(2,1)}, u32[]{:S(2)}) copy-start(bf16[128,64]{0,1:T(8,128)(2,1)} %param.16) | copy-start | bytes 49156
  0.0 83.8 %copy-start.6 = (bf16[128,64]{0,1:T(8,128)(2,1)S(1)}, bf16[128,64]{0,1:T(8,128)(2,1)}, u32[]{:S(2)}) copy-start(bf16[128,64]{0,1:T(8,128)(2,1)} %param.15) | copy-start | bytes 49156
  5.4 102.7 %collective-permute-start.2 = (bf16[16,256,128]{2,1,0:T(8,128)(2,1)}, bf16[16,256,128]{2,1,0:T(8,128)(2,1)S(1)}, u32[]{:S(2)}, u32[]{:S(2)}) collective-permute-start(bf16[16,256,128]{2,1,0:T(8,128)(2,1)} %get-tuple-element.34.n0), channel_id=1, source_target_pairs={{0,2},{2,4},{4,6},{6,0},{1,3},{3,5},{5,7},{7,1},{8,10},{10,12},{12... | collective-permute-start | bytes 3145736 | tf_op jit(solution)/shard_map/ppermute | solution.py:323
  9.5 108.4 %collective-permute-start.3 = (bf16[16,256,128]{2,1,0:T(8,128)(2,1)}, bf16[16,256,128]{2,1,0:T(8,128)(2,1)S(1)}, u32[]{:S(2)}, u32[]{:S(2)}) collective-permute-start(bf16[16,256,128]{2,1,0:T(8,128)(2,1)} %get-tuple-element.34.n0), channel_id=1, source_target_pairs={{0,6},{2,0},{4,2},{6,4},{1,7},{3,1},{5,3},{7,5},{8,14},{10,8},{12,... | collective-permute-start | bytes 3145736 | tf_op jit(solution)/shard_map/ppermute | solution.py:324
  81.3 54.9 %collective-permute-start.6 = (bf16[16,256,128]{2,1,0:T(8,128)(2,1)}, bf16[16,256,128]{2,1,0:T(8,128)(2,1)}, u32[]{:S(2)}, u32[]{:S(2)}) collective-permute-start(bf16[16,256,128]{2,1,0:T(8,128)(2,1)} %get-tuple-element.34.n0), channel_id=1, source_target_pairs={{0,4},{2,6},{4,0},{6,2},{1,5},{3,7},{5,1},{7,3},{8,12},{10,14},{12... | collective-permute-start | bytes 3145736 | tf_op jit(solution)/shard_map/ppermute | solution.py:338
  84.0 47.3 %collective-permute-start.7 = (bf16[128,512]{1,0:T(8,128)(2,1)S(1)}, bf16[128,512]{1,0:T(8,128)(2,1)S(1)}, u32[]{:S(2)}, u32[]{:S(2)}) collective-permute-start(bf16[128,512]{1,0:T(8,128)(2,1)S(1)} %concatenate.17.mine), channel_id=1, source_target_pairs={{0,1},{1,0},{2,3},{3,2},{4,5},{5,4},{6,7},{7,6},{8,9},{9,8},{10,11... | collective-permute-start | bytes 393224 | tf_op jit(solution)/shard_map/ppermute | solution.py:336
  106.2 15.7 %collective-permute-start = (bf16[4,2,32,256]{3,2,1,0:T(8,128)(2,1)S(1)}, bf16[4,2,32,256]{3,2,1,0:T(8,128)(2,1)S(1)}, u32[]{:S(2)}, u32[]{:S(2)}) collective-permute-start(bf16[4,2,32,256]{3,2,1,0:T(8,128)(2,1)S(1)} %all_to_all.5), channel_id=1, source_target_pairs={{0,24},{8,32},{16,40},{24,48},{32,56},{40,64},{48,72},{56,80},{64,... | collective-permute-start | bytes 393224 | tf_op jit(solution)/shard_map/ppermute | solution.py:329
  108.1 18.1 %collective-permute-start.1 = (bf16[4,2,32,256]{3,2,1,0:T(8,128)(2,1)S(1)}, bf16[4,2,32,256]{3,2,1,0:T(8,128)(2,1)S(1)}, u32[]{:S(2)}, u32[]{:S(2)}) collective-permute-start(bf16[4,2,32,256]{3,2,1,0:T(8,128)(2,1)S(1)} %all_to_all.5), channel_id=1, source_target_pairs={{0,232},{8,240},{16,248},{24,0},{32,8},{40,16},{48,24},{56,32},{64... | collective-permute-start | bytes 393224 | tf_op jit(solution)/shard_map/ppermute | solution.py:330
  118.0 1.2 copy-start.1
  126.3 15.5 %collective-permute-start.4 = (bf16[3,4,2,32,256]{4,3,2,1,0:T(8,128)(2,1)S(1)}, bf16[3,4,2,32,256]{4,3,2,1,0:T(8,128)(2,1)S(1)}, u32[]{:S(2)}, u32[]{:S(2)}) collective-permute-start(bf16[3,4,2,32,256]{4,3,2,1,0:T(8,128)(2,1)S(1)} %pad_maximum_fusion.rest_4_), channel_id=1, source_target_pairs={{0,8},{8,16},{16,24},{24,32},{32,40},{40,48},{48,56},{56,64},{64,7... | collective-permute-start | bytes 1179656 | tf_op jit(solution)/shard_map/ppermute | solution.py:344
  128.7 28.3 %collective-permute-start.8 = (bf16[3,4,2,32,256]{4,3,2,1,0:T(8,128)(2,1)S(1)}, bf16[3,4,2,32,256]{4,3,2,1,0:T(8,128)(2,1)S(1)}, u32[]{:S(2)}, u32[]{:S(2)}) collective-permute-start(bf16[3,4,2,32,256]{4,3,2,1,0:T(8,128)(2,1)S(1)} %pad_maximum_fusion.rest_4_), channel_id=1, source_target_pairs={{0,1},{1,0},{2,3},{3,2},{4,5},{5,4},{6,7},{7,6},{8,9},{9,8},{10,11... | collective-permute-start | bytes 1179656 | tf_op jit(solution)/shard_map/ppermute | solution.py:352
  131.4 10.4 %collective-permute-start.5 = (bf16[2,4,2,32,256]{4,3,2,1,0:T(8,128)(2,1)S(1)}, bf16[2,4,2,32,256]{4,3,2,1,0:T(8,128)(2,1)S(1)}, u32[]{:S(2)}, u32[]{:S(2)}) collective-permute-start(bf16[2,4,2,32,256]{4,3,2,1,0:T(8,128)(2,1)S(1)} %pad_maximum_fusion.1), channel_id=1, source_target_pairs={{0,248},{8,0},{16,8},{24,16},{32,24},{40,32},{48,40},{56,48},{64,5... | collective-permute-start | bytes 786440 | tf_op jit(solution)/shard_map/ppermute | solution.py:345
  141.9 15.2 %collective-permute-start.9 = (bf16[5,4,2,32,256]{4,3,2,1,0:T(8,128)(2,1)S(1)}, bf16[5,4,2,32,256]{4,3,2,1,0:T(8,128)(2,1)S(1)}, u32[]{:S(2)}, u32[]{:S(2)}) collective-permute-start(bf16[5,4,2,32,256]{4,3,2,1,0:T(8,128)(2,1)S(1)} %constant_dynamic-update-slice_fusion.rest_5_), channel_id=1, source_target_pairs={{0,1},{1,0},{2,3},{3,2},{4,5},{5,4},{6,7},{7,6},{8,9},{9,8},{10,11... | collective-permute-start | bytes 1966088 | tf_op jit(solution)/shard_map/ppermute | solution.py:353
  144.9 12.2 %copy-start.2 = (bf16[128,128]{1,0:T(8,128)(2,1)S(1)}, bf16[128,128]{1,0:T(8,128)(2,1)}, u32[]{:S(2)}) copy-start(bf16[128,128]{1,0:T(8,128)(2,1)} %rest_5_.1) | copy-start | bytes 98308
  170.2 3.8 %collective-permute-start.10 = (bf16[16,128,128]{2,1,0:T(8,128)(2,1)S(1)}, bf16[16,128,128]{2,1,0:T(8,128)(2,1)S(1)}, u32[]{:S(2)}, u32[]{:S(2)}) collective-permute-start(bf16[16,128,128]{2,1,0:T(8,128)(2,1)S(1)} %get-tuple-element.50), channel_id=1, source_target_pairs={{0,1},{1,0},{2,3},{3,2},{4,5},{5,4},{6,7},{7,6},{8,9},{9,8},{10,11... | collective-permute-start | bytes 1572872 | tf_op jit(solution)/shard_map/ppermute | solution.py:364
